TPU v7x, 256 devices: a whole 4x4x8 slice. The times are simulated.
256 devices in a mesh: row: 8 (over z), col: 32 (over x, y, core).
Axes of the slice: x: 4, y: 4, z: 8, core: 2. Of those that a mesh axis runs over, the one named last changes fastest.
Arguments:
- gradient: bfloat16 [28672, 8192], P('row', 'col'), may hold values from -6 to 6
- projector: bfloat16 [8192, 1024], P('col', 'row'), may hold values from -0.0625 to 0.0625
- first_moment: float32 [1024, 28672], P('col', 'row'), may hold values from -2 to 2
- second_moment: float32 [1024, 28672], P('col', 'row'), may hold values from 0.0001 to 0.01
Outputs:
- update: float32 [28672, 8192], P('row', 'col')
- first_next: float32 [1024, 28672], P('col', 'row')
- second_next: float32 [1024, 28672], P('col', 'row')
All inputs are finite; a program needn't handle non-finite values.
Results may differ from a plain program's by a relative error of at most 0.0058.
Values may be sent and summed in bfloat16 or wider, within the bound.
No kernel may reach another device: no remote copies, remote signals or barrier semaphores. Data moves between devices by JAX's collectives and lax.ppermute only.
A program may use at most 64 MiB of HBM per device.

v0:
```python
import jax
import jax.numpy as jnp
from jax import lax
from jax.sharding import PartitionSpec as P


def in_order(pieces, dim):
    lengths = list(pieces.shape[1:])
    lengths[dim] *= pieces.shape[0]
    return jnp.moveaxis(pieces, 0, dim).reshape(lengths)


def sent_to_all(x, axis):
    peers = lax.axis_size(axis)
    return lax.all_to_all(jnp.broadcast_to(x[None], (peers, *x.shape)), axis, 0, 0, tiled=True)


def gathered_copies(x, axis, dim):
    return in_order(sent_to_all(x, axis), dim)


def in_blocks(x, dim, peers):
    before, after = (x.shape[:dim], x.shape[dim + 1 :])
    return jnp.moveaxis(x.reshape(*before, peers, -1, *after), dim, 0)


def sum_at_owner(x, axis, dim):
    peers = lax.axis_size(axis)
    pieces = lax.all_to_all(in_blocks(x, dim, peers), axis, 0, 0, tiled=True)
    return jnp.sum(pieces.astype(jnp.float32), axis=0)


def adam_moments(compressed, first_moment, second_moment):
    first_next = 0.9 * first_moment + 0.1 * compressed
    second_next = 0.999 * second_moment + 0.001 * compressed * compressed
    corr_first = 1.0 - 0.9**10
    corr_second = 1.0 - 0.999**10
    direction = (first_next / corr_first / (jnp.sqrt(second_next / corr_second) + 1e-08)).astype(
        jnp.bfloat16
    )
    return (direction, first_next, second_next)


def shards(gradient, projector, first_moment, second_moment):
    proj_rows = gathered_copies(projector, "row", 1)
    proj_part = proj_rows
    compressed = sum_at_owner(
        lax.dot_general(
            proj_part, gradient, (((0,), (1,)), ((), ())), preferred_element_type=jnp.float32
        ).astype(jnp.bfloat16),
        "col",
        0,
    )
    direction, first_next, second_next = adam_moments(compressed, first_moment, second_moment)
    proj_part = proj_rows
    update = lax.dot_general(
        lax.all_gather(direction, "col", axis=0, tiled=True),
        proj_part,
        (((0,), (1,)), ((), ())),
        preferred_element_type=jnp.float32,
    )
    return (update, first_next, second_next)


def solution(mesh):
    return jax.shard_map(
        shards,
        mesh=mesh,
        in_specs=(P("row", "col"), P("col", "row"), P("col", "row"), P("col", "row")),
        out_specs=(P("row", "col"), P("col", "row"), P("col", "row")),
        check_vma=False,
    )
```

profile of v0, /device:TPU:1, one launch (start us, length us, event | category | flops | bytes accessed | tf_op | source)
XLA Modules:
  0.0 193.9 jit_solution(3954843862253366872)
XLA Ops:
  7.2 0.0 copy-start
  7.2 0.0 all-gather.2.cloned.1.call-start
  7.2 1.1 copy.7
  8.3 24.9 %all_to_all.10 = bf16[8,256,128]{1,2,0:T(8,128)(2,1)S(1)} all-to-all(bf16[8,256,128]{1,2,0:T(8,128)(2,1)S(1)} %broadcast_in_dim.2), channel_id=1, replica_groups=mesh['row'=8,'col'=32] {'row'}, dimensions={0} | all-to-all | bytes 1048576 | tf_op jit(solution)/shard_map/all_to_all | solution.py:15
  33.3 0.0 copy-done
  33.3 2.1 %convolution_convert_fusion = bf16[1024,3584]{1,0:T(8,128)(2,1)S(1)} fusion(bf16[256,1024]{0,1:T(8,128)(2,1)S(1)} %bitcast.9, bf16[3584,256]{1,0:T(8,128)(2,1)S(1)} %copy-done), kind=kOutput, calls=%fused_computation.1 | convolution fusion | flops 1882718208 | bytes 9699328 | tf_op jit(solution)/shard_map/dot_general | solution.py:48
  35.4 93.5 %all_to_all.11 = bf16[32,32,3584]{2,1,0:T(8,128)(2,1)S(1)} all-to-all(bf16[32,32,3584]{2,1,0:T(8,128)(2,1)S(1)} %bitcast.8), channel_id=1, replica_groups=mesh['row'=8,'col'=32] {'col'}, dimensions={0} | all-to-all | bytes 14680064 | tf_op jit(solution)/shard_map/all_to_all | solution.py:29
  128.9 0.0 copy-start.1
  128.9 0.0 copy-start.2
  128.9 1.0 convert_reduce_fusion
  129.9 0.0 copy-done.1
  130.0 0.1 copy-done.2
  130.1 1.1 divide_convert_fusion
  131.2 0.0 all-gather.2.cloned.1.call-update
  131.2 48.8 %all-gather.2.cloned.1.call-done = bf16[1024,3584]{1,0:T(8,128)(2,1)} async-done(((bf16[32,3584]{1,0:T(8,128)(2,1)}), bf16[1024,3584]{1,0:T(8,128)(2,1)}) %all-gather.2.cloned.1.call-update) | async-done | bytes 7340048 | tf_op jit(solution)/shard_map/all_gather | solution.py:57
  180.1 7.0 %fusion.2 = f32[3584,256]{1,0:T(8,128)} fusion(bf16[1024,3584]{1,0:T(8,128)(2,1)} %all-gather.2.cloned.1.call-done, bf16[256,1024]{0,1:T(8,128)(2,1)S(1)} %bitcast.10), kind=kOutput, calls=%fused_computation.6 | convolution fusion | flops 1879048192 | bytes 11534336 | tf_op jit(solution)/shard_map/dot_general | solution.py:56
  (1 shorter events, 0.0 us)
Async XLA Ops:
  7.2 26.1 %copy-start = (bf16[3584,256]{1,0:T(8,128)(2,1)S(1)}, bf16[3584,256]{1,0:T(8,128)(2,1)}, u32[]{:S(2)}) copy-start(bf16[3584,256]{1,0:T(8,128)(2,1)} %param.4) | copy-start | bytes 5505028
  7.2 172.9 %all-gather.2.cloned.1.call-start = ((), (), s32[]{:S(2)}) async-start(), calls=%async_computation.2 | async-start | bytes 7569408 | tf_op jit(solution)/shard_map/all_gather | solution.py:57
  128.9 1.0 copy-start.1
  128.9 1.2 copy-start.2
Sparse Core Ops, SparseCore 0:
  131.4 48.6 all-gather.1
where the time goes:
time: 194 us
  blocking collectives  118 us (61%)
  waiting for transfers between devices  48.8 us (25%)
  between operations  14.1 us (7%)
  matrix products  9.14 us (5%)
  other arithmetic  2.17 us (1%)
    all_to_all x1, blocking collectives, sum_at_owner(): pieces = lax.all_to_all(in_blocks(x, dim, peers), axis, 0, 0, tiled=True)  93.5 us
    all_gather x1, waiting for transfers between devices, shards(): lax.all_gather(direction, 'col', axis=0, tiled=True)  48.8 us
    all_to_all x1, blocking collectives, sent_to_all(): lax.all_to_all(jnp.broadcast_to(x[None], (peers, *x.shape)), axis, 0, 0,...  24.9 us
    dot_general x1, matrix products, shards(): lax.dot_general(lax.all_gather(direction, 'col', axis=0, tiled=True), pro...  7.03 us
  transfers between devices with their start and end apart: 1, of which 1 were waited for; matrix products, arithmetic and copies ran while one was open for 0% of the time, Pallas kernels for 0%

commit v1 on v0

--- a/solution.py
+++ b/solution.py
@@ -2,6 +2,18 @@
 import jax.numpy as jnp
 from jax import lax
 from jax.sharding import PartitionSpec as P
+
+
+def gather_by_bits(array, axis, dim):
+    ways, here = (lax.axis_size(axis), lax.axis_index(axis))
+    grown, reach = (array, 1)
+    while reach < ways:
+        theirs = lax.ppermute(grown, axis, [(d, d ^ reach) for d in range(ways)])
+        mine_first = jnp.concatenate([grown, theirs], axis=dim)
+        theirs_first = jnp.concatenate([theirs, grown], axis=dim)
+        grown = jnp.where(here & reach == 0, mine_first, theirs_first)
+        reach = 2 * reach
+    return grown
 
 
 def in_order(pieces, dim):
@@ -54,7 +66,7 @@
     direction, first_next, second_next = adam_moments(compressed, first_moment, second_moment)
     proj_part = proj_rows
     update = lax.dot_general(
-        lax.all_gather(direction, "col", axis=0, tiled=True),
+        gather_by_bits(direction, "col", 0),
         proj_part,
         (((0,), (1,)), ((), ())),
         preferred_element_type=jnp.float32,

time: 194 us -> 300 us (1.55)
  waiting for transfers between devices: 48.8 us -> 153 us
  between operations: 14.1 us -> 0.71 us
  other arithmetic: 2.17 us -> 12.1 us
    ppermute x0 -> x5, waiting for transfers between devices: none -> 153 us  [gather_by_bits(): theirs = lax.ppermute(grown, axis, [(d, d ^ reach) for d in range(ways)])]
    all_gather x1 -> x0, waiting for transfers between devices: 48.8 us -> none  [shards(): lax.all_gather(direction, 'col', axis=0, tiled=True)]
    select_n x0 -> x4, other arithmetic: none -> 9.85 us  [gather_by_bits(): grown = jnp.where(here & reach == 0, mine_first, theirs_first)]
  transfers between devices with their start and end apart: 1 -> 5, of which waited for: 1 -> 5; matrix products, arithmetic and copies ran while one was open for 0% -> 0% of each run, Pallas kernels for 0% -> 0%
where the time goes in v1:
time: 300 us; the launch traced here: 299 us
  waiting for transfers between devices  153 us (51%)
  blocking collectives  118 us (39%)
  other arithmetic  12.1 us (4%)
  matrix products  9.92 us (3%)
    ppermute x5, waiting for transfers between devices, gather_by_bits(): theirs = lax.ppermute(grown, axis, [(d, d ^ reach) for d in range(ways)])  153 us
    all_to_all x1, blocking collectives, sum_at_owner(): pieces = lax.all_to_all(in_blocks(x, dim, peers), axis, 0, 0, tiled=True)  93.5 us
    all_to_all x1, blocking collectives, sent_to_all(): lax.all_to_all(jnp.broadcast_to(x[None], (peers, *x.shape)), axis, 0, 0,...  24.9 us
    select_n x4, other arithmetic, gather_by_bits(): grown = jnp.where(here & reach == 0, mine_first, theirs_first)  9.85 us
    dot_general x1, matrix products, shards(): lax.dot_general(gather_by_bits(direction, 'col', 0), proj_part, (((0,), (...  7.81 us
  transfers between devices with their start and end apart: 5, of which 5 were waited for; matrix products, arithmetic and copies ran while one was open for 0% of the time, Pallas kernels for 0%

profile of v1, /device:TPU:1, one launch (start us, length us, event | category | flops | bytes accessed | tf_op | source)
XLA Modules:
  0.0 298.7 jit_solution(13951542499649732398)
XLA Ops:
  0.6 0.0 copy-start
  0.6 1.1 copy.7
  1.8 24.9 %all_to_all.10 = bf16[8,256,128]{1,2,0:T(8,128)(2,1)S(1)} all-to-all(bf16[8,256,128]{1,2,0:T(8,128)(2,1)S(1)} %broadcast_in_dim.2), channel_id=1, replica_groups=mesh['row'=8,'col'=32] {'row'}, dimensions={0} | all-to-all | bytes 1048576 | tf_op jit(solution)/shard_map/all_to_all | solution.py:27
  26.7 0.0 copy-done
  26.7 2.1 convolution_convert_fusion
  28.8 93.5 %all_to_all.11 = bf16[32,32,3584]{2,1,0:T(8,128)(2,1)S(1)} all-to-all(bf16[32,32,3584]{2,1,0:T(8,128)(2,1)S(1)} %bitcast.7), channel_id=1, replica_groups=mesh['row'=8,'col'=32] {'col'}, dimensions={0} | all-to-all | bytes 14680064 | tf_op jit(solution)/shard_map/all_to_all | solution.py:41
  122.3 0.0 copy-start.2
  122.3 0.0 copy-start.3
  122.3 1.0 convert_reduce_fusion
  123.4 0.0 copy-done.2
  123.4 0.1 copy-done.3
  123.5 1.2 divide_convert_fusion
  124.7 0.1 collective-permute-start
  124.8 1.4 collective-permute-done
  126.2 0.1 maximum_select_fusion.5
  126.3 0.0 copy-start.1
  126.3 0.1 collective-permute-start.1
  126.4 0.7 copy-done.1
  127.0 11.4 %collective-permute-done.1 = bf16[64,3584]{1,0:T(8,128)(2,1)} collective-permute-done((bf16[64,3584]{1,0:T(8,128)(2,1)S(1)}, bf16[64,3584]{1,0:T(8,128)(2,1)}, u32[]{:S(2)}, u32[]{:S(2)}) %collective-permute-start.1) | collective-permute-done | bytes 458784 | tf_op jit(solution)/shard_map/ppermute | solution.py:11
  138.4 1.6 maximum_select_fusion.4
  140.1 1.1 collective-permute-start.2
  141.2 21.5 %collective-permute-done.2 = bf16[128,3584]{1,0:T(8,128)(2,1)} collective-permute-done((bf16[128,3584]{1,0:T(8,128)(2,1)S(1)}, bf16[128,3584]{1,0:T(8,128)(2,1)}, u32[]{:S(2)}, u32[]{:S(2)}) %collective-permute-start.2) | collective-permute-done | bytes 917536 | tf_op jit(solution)/shard_map/ppermute | solution.py:11
  162.7 3.1 %maximum_select_fusion.3 = bf16[256,3584]{1,0:T(8,128)(2,1)} fusion(bf16[128,3584]{1,0:T(8,128)(2,1)} %collective-permute-done.2, bf16[128,3584]{1,0:T(8,128)(2,1)S(1)} %maximum_select_fusion.4, pred[]{:T(512)S(6)} %eq.17), kind=kLoop, calls=%fused_computation.11 | loop fusion | flops 8257536 | bytes 3670017 | tf_op jit(solution)/shard_map/jit(_where)/select_n | solution.py:14
  165.8 0.0 collective-permute-start.3
  165.8 40.0 %collective-permute-done.3 = bf16[256,3584]{1,0:T(8,128)(2,1)} collective-permute-done((bf16[256,3584]{1,0:T(8,128)(2,1)}, bf16[256,3584]{1,0:T(8,128)(2,1)}, u32[]{:S(2)}, u32[]{:S(2)}) %collective-permute-start.3) | collective-permute-done | bytes 1835040 | tf_op jit(solution)/shard_map/ppermute | solution.py:11
  205.9 5.0 %maximum_select_fusion.2 = bf16[512,3584]{1,0:T(8,128)(2,1)} fusion(bf16[256,3584]{1,0:T(8,128)(2,1)} %collective-permute-done.3, bf16[256,3584]{1,0:T(8,128)(2,1)} %maximum_select_fusion.3, pred[]{:T(512)S(6)} %eq.16), kind=kLoop, calls=%fused_computation.10 | loop fusion | flops 16515072 | bytes 7340033 | tf_op jit(solution)/shard_map/jit(_where)/select_n | solution.py:14
  210.8 1.2 collective-permute-start.4
  212.1 78.8 %collective-permute-done.4 = bf16[512,3584]{1,0:T(8,128)(2,1)} collective-permute-done((bf16[512,3584]{1,0:T(8,128)(2,1)}, bf16[512,3584]{1,0:T(8,128)(2,1)}, u32[]{:S(2)}, u32[]{:S(2)}) %collective-permute-start.4) | collective-permute-done | bytes 3670048 | tf_op jit(solution)/shard_map/ppermute | solution.py:11
  290.9 7.8 %fusion = f32[3584,256]{1,0:T(8,128)} fusion(bf16[256,1024]{0,1:T(8,128)(2,1)S(1)} %bitcast.9, bf16[512,3584]{1,0:T(8,128)(2,1)} %collective-permute-done.4, bf16[512,3584]{1,0:T(8,128)(2,1)} %maximum_select_fusion.2, pred[]{:T(512)S(6)} %eq.15), kind=kOutput, calls=%fused_computation.3 | convolution fusion | flops 1912078336 | bytes 11534337 | tf_op jit(solution)/shard_map/dot_general | solution.py:68
  (1 shorter events, 0.0 us)
Async XLA Ops:
  0.6 26.1 %copy-start = (bf16[3584,256]{1,0:T(8,128)(2,1)S(1)}, bf16[3584,256]{1,0:T(8,128)(2,1)}, u32[]{:S(2)}) copy-start(bf16[3584,256]{1,0:T(8,128)(2,1)} %param.4) | copy-start | bytes 5505028
  122.3 1.0 copy-start.2
  122.3 1.2 copy-start.3
  124.7 1.5 collective-permute-start
  126.3 0.8 copy-start.1
  126.3 12.1 %collective-permute-start.1 = (bf16[64,3584]{1,0:T(8,128)(2,1)S(1)}, bf16[64,3584]{1,0:T(8,128)(2,1)}, u32[]{:S(2)}, u32[]{:S(2)}) collective-permute-start(bf16[64,3584]{1,0:T(8,128)(2,1)S(1)} %maximum_select_fusion.5), channel_id=1, source_target_pairs={{0,2},{1,3},{2,0},{3,1},{4,6},{5,7},{6,4},{7,5},{8,10},{9,11},{10,... | collective-permute-start | bytes 1376264 | tf_op jit(solution)/shard_map/ppermute | solution.py:11
  140.1 22.6 %collective-permute-start.2 = (bf16[128,3584]{1,0:T(8,128)(2,1)S(1)}, bf16[128,3584]{1,0:T(8,128)(2,1)}, u32[]{:S(2)}, u32[]{:S(2)}) collective-permute-start(bf16[128,3584]{1,0:T(8,128)(2,1)S(1)} %maximum_select_fusion.4), channel_id=1, source_target_pairs={{0,4},{1,5},{2,6},{3,7},{4,0},{5,1},{6,2},{7,3},{8,12},{9,13},{10,... | collective-permute-start | bytes 2752520 | tf_op jit(solution)/shard_map/ppermute | solution.py:11
  165.8 40.0 %collective-permute-start.3 = (bf16[256,3584]{1,0:T(8,128)(2,1)}, bf16[256,3584]{1,0:T(8,128)(2,1)}, u32[]{:S(2)}, u32[]{:S(2)}) collective-permute-start(bf16[256,3584]{1,0:T(8,128)(2,1)} %maximum_select_fusion.3), channel_id=1, source_target_pairs={{0,8},{1,9},{2,10},{3,11},{4,12},{5,13},{6,14},{7,15},{8,0},{9,1},... | collective-permute-start | bytes 5505032 | tf_op jit(solution)/shard_map/ppermute | solution.py:11
  210.8 80.0 %collective-permute-start.4 = (bf16[512,3584]{1,0:T(8,128)(2,1)}, bf16[512,3584]{1,0:T(8,128)(2,1)}, u32[]{:S(2)}, u32[]{:S(2)}) collective-permute-start(bf16[512,3584]{1,0:T(8,128)(2,1)} %maximum_select_fusion.2), channel_id=1, source_target_pairs={{0,16},{1,17},{2,18},{3,19},{4,20},{5,21},{6,22},{7,23},{8,24},{9,... | collective-permute-start | bytes 11010056 | tf_op jit(solution)/shard_map/ppermute | solution.py:11
